TPU v7x, 256 devices: a whole 4x4x8 slice. The times are simulated.
256 devices in a mesh: gz: 32 (over z, x_lo, core), gx: 2 (over x_hi), gy: 4 (over y).
Axes of the slice: x: 4 (x_hi: 2, x_lo: 2; x = x_hi * 2 + x_lo), y: 4, z: 8, core: 2. Of those that a mesh axis runs over, the one named last changes fastest.
Arguments:
- density: float32 [128, 256, 4096], P('gx', 'gy', 'gz'), may hold values from 0.01 to 1
- design_mask: int32 [128, 256, 4096], P('gx', 'gy', 'gz'), may hold values from 0 to 2
- energy: bfloat16 [4, 128, 256, 4096], P(None, 'gx', 'gy', 'gz'), may hold values from 0.099609375 to 3
- decay: float32 [4, 4096], P(None, 'gz'), may hold values from 0.3 to 1
- case_index: int32 [4], replicated, may hold values from 0 to 15
- case_weight: float32 [16], replicated, may hold values from 0.2 to 1
Outputs:
- sensitivity: float32 [128, 256, 4096], P('gx', 'gy', 'gz')
- compliance: float32 [4], replicated
All inputs are finite; a program needn't handle non-finite values.
Results may differ from a plain program's by a relative error of at most 0.0006.
Values may be sent and summed in bfloat16 or wider, within the bound.
A program may use at most 128 MiB of HBM per device.

v0:
```python
import functools
import math

import jax
import jax.numpy as jnp
from jax import lax
from jax.experimental import pallas as pl
from jax.experimental.pallas import tpu as pltpu
from jax.sharding import PartitionSpec as P

CASES = 4
RADIUS = 3
F32 = jnp.float32
BF16 = jnp.bfloat16
MESH = pl.DeviceIdType.MESH
HIGH = lax.Precision.HIGHEST
XG = 8
YO = 8

_raw = [math.exp(-2.0 * k * k / (RADIUS * RADIUS)) for k in range(-RADIUS, RADIUS + 1)]
TAPS = [t / sum(_raw) for t in _raw]


def dot(a, b, ca, cb, precision=None):
    return lax.dot_general(a, b, (((ca,), (cb,)), ((), ())), precision=precision, preferred_element_type=F32)


def split(value):
    hi = value.astype(BF16)
    return hi, (value - hi.astype(F32)).astype(BF16)


def kernel(
    sizes, dens_hbm, mask_hbm, en_hbm, decay_ref, index_ref, weight_ref,
    out_hbm, comp_out,
    dens, mask, en, scale, lhs, maps, coef, vmap, ext, tmp, out,
    consts_out, consts_in, fh_out, fh_in, fin, carry_out, carry_in,
    cs_out, cs_in, ct_out, ct_in, xs_out, xs_in, ys_out, ys_in, ds_out, ds_in,
    load_sem, out_sem, cst_s, cst_r, ph1_s, ph1_r, ph2_s, ph2_r, cs_s, cs_r, ct_s, ct_r,
    xs_s, xs_r, ys_s, ys_r, ds_s, ds_r,
):
    n, ngx, ngy, lx, ly, lz, cells = sizes
    groups = lx // XG
    per = XG * ly
    gz, gx, gy = lax.axis_index("gz"), lax.axis_index("gx"), lax.axis_index("gy")
    others = ngx * ngy - 1

    def peer(k):
        flat = lax.rem(gx * ngy + gy + 1 + k, ngx * ngy)
        return {"gz": gz, "gx": flat // ngy, "gy": lax.rem(flat, ngy)}

    barrier = pltpu.get_barrier_semaphore()

    def greet(k, _):
        pl.semaphore_signal(barrier, inc=1, device_id={"gz": lax.rem(gz + k, n)}, device_id_type=MESH)
        return 0

    lax.fori_loop(1, n, greet, 0)
    for k in range(others):
        pl.semaphore_signal(barrier, inc=1, device_id=peer(k), device_id_type=MESH)

    def loads(k):
        rows = pl.ds(k * XG, XG)
        return (
            pltpu.make_async_copy(dens_hbm.at[rows], dens.at[rows], load_sem.at[0, k]),
            pltpu.make_async_copy(mask_hbm.at[rows], mask.at[rows], load_sem.at[1, k]),
            pltpu.make_async_copy(en_hbm.at[:, rows], en.at[:, rows], load_sem.at[2, k]),
        )

    def start_loads(k, _):
        for copy in loads(k):
            copy.start()
        return 0

    lax.fori_loop(0, groups, start_loads, 0)

    decay = jnp.concatenate([decay_ref[...], decay_ref[...]], axis=0)
    logs = jnp.log(decay)
    row = lax.broadcasted_iota(jnp.int32, (lz, lz), 0)
    col = lax.broadcasted_iota(jnp.int32, (lz, lz), 1)
    up = dot(logs, (row <= col).astype(F32), 1, 0, HIGH)
    down = dot(logs, (row >= col).astype(F32), 1, 0, HIGH)
    keep = 1.0 - decay
    columns = jnp.transpose(jnp.concatenate([up, down, keep, keep], axis=0))
    total = up[:, lz - 1 : lz]
    fwd_last = jnp.exp(total - up) * keep
    first = jnp.exp(down[:, 0:1] - down) * keep
    lead = jnp.exp(up)
    trail = jnp.exp(down)
    maps[...] = jnp.zeros_like(maps)
    coef[...] = jnp.zeros_like(coef)
    rows8 = lax.broadcasted_iota(jnp.int32, (8, lz), 0)
    cblock = jnp.zeros((8, lz), F32)
    vals = jnp.zeros((8, lz), F32)
    couple = jnp.zeros((8, lz), F32)
    for c in range(CASES):
        wc = weight_ref[index_ref[c]] * -3.0
        up_col, down_col, keep_col = columns[:, c : c + 1], columns[:, 8 + c : 9 + c], columns[:, 16 + c : 17 + c]
        low = row <= col
        fwd_t = jnp.where(low, jnp.exp(jnp.where(low, up[c : c + 1] - up_col, 0.0)), 0.0) * keep_col
        high = row >= col
        bwd_t = jnp.where(high, jnp.exp(jnp.where(high, down[c : c + 1] - down_col, 0.0)), 0.0) * keep_col
        both = dot(fwd_t, bwd_t, 1, 0, HIGH) * wc
        hi, lo = split(both)
        for half in range(2):
            at = (2 * c + half) * lz
            maps[at : at + lz, 0:lz] = hi
            maps[at : at + lz, lz : 2 * lz] = lo
        hrow = dot(first, fwd_t, 1, 1, HIGH)
        lead_map = dot(lead, bwd_t, 1, 0, HIGH)
        cblock = jnp.where(rows8 == c, fwd_last, 0.0)
        cblock = jnp.where(rows8 == c + CASES, hrow, cblock)
        chi = cblock.astype(BF16).astype(F32)
        pair = jnp.concatenate([chi, cblock - chi], axis=0).astype(BF16)
        for half in range(2):
            at = (2 * c + half) * lz
            coef[:, at : at + lz] = pair
        vals = jnp.where(rows8 == c, lead_map * wc, vals)
        vals = jnp.where(rows8 == c + CASES, trail * wc, vals)
        couple = jnp.where((rows8 == c) | (rows8 == c + CASES), jnp.broadcast_to(lead_map[:, 0:1], (8, lz)), couple)
    vhi = vals.astype(BF16).astype(F32)
    vmap[...] = jnp.concatenate([vhi, vhi, vals - vhi, jnp.zeros((8, lz), F32)], axis=0).astype(BF16)
    consts_out[0:8] = jnp.broadcast_to(jnp.exp(total), (8, lz))
    consts_out[8:16] = couple
    consts_in[gz] = consts_out[...]

    pl.semaphore_wait(barrier, n - 1 + others)

    def to_slab(src, dst, send, recv, k):
        return pltpu.make_async_remote_copy(
            src_ref=src, dst_ref=dst, send_sem=send, recv_sem=recv,
            device_id={"gz": k}, device_id_type=MESH,
        )

    def consts_copy(src, dst):
        return to_slab(consts_out, consts_in.at[src], cst_s.at[dst], cst_r.at[src], dst)

    def ph1_copy(src, dst):
        return to_slab(fh_out.at[dst], fh_in.at[src], ph1_s.at[dst], ph1_r.at[src], dst)

    def ph2_copy(src, dst):
        return to_slab(carry_out.at[dst], carry_in.at[src], ph2_s.at[dst], ph2_r.at[src], dst)

    def ct_copy(src, dst):
        return to_slab(ct_out, ct_in.at[src], ct_s.at[dst], ct_r.at[src], dst)

    def send_consts(k, _):
        consts_copy(gz, lax.rem(gz + k, n)).start()
        return 0

    lax.fori_loop(1, n, send_consts, 0)

    ext[...] = jnp.zeros_like(ext)

    def local(k, sums):
        for copy in loads(k):
            copy.wait()
        sums = list(sums)
        for i in range(XG):
            x = k * XG + i
            d, m = dens[x], mask[x]
            dense = jnp.where(m == 1, 0.001, jnp.where(m == 2, 1.0, d))
            cube = dense * dense * dense
            scale[x] = jnp.where(m == 0, 1.0 / jnp.maximum(d, 0.1), 0.0)
            for c in range(CASES):
                g = cube * en[c, x].astype(F32)
                sums[c] = sums[c] + jnp.sum(g.reshape(ly // 8, 8, lz), axis=0)
                hi, lo = split(g)
                lhs[i * ly : (i + 1) * ly, 2 * c * lz : (2 * c + 1) * lz] = hi
                lhs[i * ly : (i + 1) * ly, (2 * c + 1) * lz : (2 * c + 2) * lz] = lo
        full = dot(lhs[...], maps[...], 1, 0)
        full = full[:, :lz] + full[:, lz:]
        ext[pl.ds(RADIUS + k * XG, XG), YO : YO + ly, :] = full.reshape(XG, ly, lz)
        fh = dot(coef[...], lhs[...], 1, 1)
        fh = fh[0:8] + fh[8:16]
        for b in range(per // lz):
            p = k * (per // lz) + b
            fh_out[p] = fh[:, b * lz : (b + 1) * lz]
        return tuple(sums)

    sums = lax.fori_loop(0, groups, local, tuple(jnp.zeros((8, lz), F32) for _ in range(CASES)))

    def send_ph1(k, _):
        ph1_copy(gz, lax.rem(gz + k, n)).start()
        return 0

    lax.fori_loop(1, n, send_ph1, 0)
    fh_in[gz] = fh_out[gz]

    cs_out[...] = jnp.concatenate([jnp.sum(s, axis=0, keepdims=True) for s in sums] * 2, axis=0)

    def cs_copy(k):
        return pltpu.make_async_remote_copy(
            src_ref=cs_out, dst_ref=cs_in.at[k], send_sem=cs_s.at[k], recv_sem=cs_r.at[k],
            device_id=peer(k), device_id_type=MESH,
        )

    for k in range(others):
        cs_copy(k).start()
    part = cs_out[...]
    for k in range(others):
        cs_copy(k).wait_recv()
        part = part + cs_in[k]
    ct_out[...] = part

    def send_ct(k, _):
        ct_copy(gz, lax.rem(gz + k, n)).start()
        return 0

    lax.fori_loop(1, n, send_ct, 0)
    ct_in[gz] = part

    def ascend(s, state):
        @pl.when(s != gz)
        def _():
            consts_copy(s, gz).wait_recv()
            ph1_copy(s, gz).wait_recv()

        fin[s] = state
        return consts_in[s, 0:8] * state + fh_in[s]

    lax.fori_loop(0, n, ascend, jnp.zeros((8, lz), F32))

    def descend(k, state):
        s = n - 1 - k
        entering = fin[s]
        carry_out[s] = jnp.where(rows8 < CASES, entering, state)

        @pl.when(s != gz)
        def _():
            ph2_copy(gz, s).start()

        turned = pltpu.roll(entering, CASES, 0)
        return consts_in[s, 0:8] * state + fh_in[s] + consts_in[s, 8:16] * turned

    lax.fori_loop(0, n, descend, jnp.zeros((8, lz), F32))
    carry_in[gz] = carry_out[gz]

    rows_per = lz // ly

    def correct(p, _):
        @pl.when(p != gz)
        def _():
            ph2_copy(p, gz).wait_recv()

        state = carry_in[p]
        hi = state.astype(BF16).astype(F32)
        stack = jnp.concatenate([hi, state - hi, hi, jnp.zeros((8, lz), F32)], axis=0)
        add = dot(jnp.transpose(stack).astype(BF16), vmap[...], 1, 0)
        at = pl.ds(RADIUS + p * rows_per, rows_per)
        ext[at, YO : YO + ly, :] = ext[at, YO : YO + ly, :] + add.reshape(rows_per, ly, lz)
        return 0

    lax.fori_loop(0, n, correct, 0)

    xs_at = jnp.where(gx == 0, lx - RADIUS, 0)
    for j in range(RADIUS):
        xs_out[j] = ext[RADIUS + xs_at + j, YO : YO + ly, :].astype(BF16)
    for side in range(2):
        for j in range(RADIUS):
            y = YO + (j if side == 0 else ly - RADIUS + j)
            ys_out[side, j] = ext[RADIUS : RADIUS + lx, y, :].astype(BF16)
            ds_out[side, j] = ext[pl.ds(RADIUS + xs_at, RADIUS), y, :].astype(BF16)

    x_copy = pltpu.make_async_remote_copy(
        src_ref=xs_out, dst_ref=xs_in, send_sem=xs_s, recv_sem=xs_r,
        device_id={"gx": 1 - gx}, device_id_type=MESH,
    )

    def y_copy(side, to):
        return pltpu.make_async_remote_copy(
            src_ref=ys_out.at[side], dst_ref=ys_in.at[1 - side], send_sem=ys_s.at[side], recv_sem=ys_r.at[1 - side],
            device_id={"gy": to}, device_id_type=MESH,
        )

    def d_copy(side, to):
        return pltpu.make_async_remote_copy(
            src_ref=ds_out.at[side], dst_ref=ds_in.at[1 - side], send_sem=ds_s.at[side], recv_sem=ds_r.at[1 - side],
            device_id={"gx": 1 - gx, "gy": to}, device_id_type=MESH,
        )

    x_copy.start()

    @pl.when(gy > 0)
    def _():
        y_copy(0, gy - 1).start()
        d_copy(0, gy - 1).start()

    @pl.when(gy < ngy - 1)
    def _():
        y_copy(1, gy + 1).start()
        d_copy(1, gy + 1).start()

    def add_ct(s, state):
        @pl.when(s != gz)
        def _():
            ct_copy(s, gz).wait_recv()

        return state + ct_in[s]

    whole = lax.fori_loop(0, n, add_ct, jnp.zeros((8, lz), F32))
    for c in range(CASES):
        comp_out[c] = jnp.sum(whole[c : c + 1]) * (1.0 / cells)

    halo_x = jnp.where(gx == 0, RADIUS + lx, 0)
    x_copy.wait()
    ext[pl.ds(halo_x, RADIUS), YO : YO + ly, :] = xs_in[...].astype(F32)

    def take(side):
        for j in range(RADIUS):
            y = YO + (j - RADIUS if side == 0 else ly + j)
            ext[RADIUS : RADIUS + lx, y, :] = ys_in[side, j].astype(F32)
            ext[pl.ds(halo_x, RADIUS), y, :] = ds_in[side, j].astype(F32)

    @pl.when(gy > 0)
    def _():
        for copy in (y_copy, d_copy):
            copy(0, gy - 1).wait_send()
            copy(1, gy - 1).wait_recv()
        take(0)

    @pl.when(gy < ngy - 1)
    def _():
        for copy in (y_copy, d_copy):
            copy(1, gy + 1).wait_send()
            copy(0, gy + 1).wait_recv()
        take(1)

    def out_copy(k):
        rows = pl.ds(k * XG, XG)
        return pltpu.make_async_copy(out.at[rows], out_hbm.at[rows], out_sem.at[k])

    def taps(get):
        acc = TAPS[RADIUS] * get(RADIUS)
        for t in range(RADIUS):
            acc = acc + TAPS[t] * (get(t) + get(2 * RADIUS - t))
        return acc

    def filtered(k, _):
        for i in range(XG):
            x = k * XG + i
            tmp[i] = taps(lambda t: ext[x + t])
            along = taps(lambda t: tmp[i, YO - RADIUS + t : YO - RADIUS + t + ly, :])
            out[x] = along * scale[x]
        out_copy(k).start()
        return 0

    lax.fori_loop(0, groups, filtered, 0)

    def drain(k, _):
        s = lax.rem(gz + k, n)
        consts_copy(gz, s).wait_send()
        ph1_copy(gz, s).wait_send()
        ph2_copy(gz, s).wait_send()
        ct_copy(gz, s).wait_send()
        return 0

    lax.fori_loop(1, n, drain, 0)
    for k in range(others):
        cs_copy(k).wait_send()

    def drain_out(k, _):
        out_copy(k).wait()
        return 0

    lax.fori_loop(0, groups, drain_out, 0)


def local_step(sizes, density, design_mask, energy, decay, case_index, case_weight):
    n, ngx, ngy, lx, ly, lz, cells = sizes
    groups = lx // XG
    per = XG * ly
    others = ngx * ngy - 1
    dma = pltpu.SemaphoreType.DMA
    anywhere = pl.BlockSpec(memory_space=pl.ANY)
    smem = pl.BlockSpec(memory_space=pltpu.SMEM)
    return pl.pallas_call(
        functools.partial(kernel, sizes),
        out_shape=(
            jax.ShapeDtypeStruct((lx, ly, lz), F32),
            jax.ShapeDtypeStruct((CASES,), F32),
        ),
        in_specs=[anywhere, anywhere, anywhere, pl.BlockSpec(memory_space=pltpu.VMEM), smem, smem],
        out_specs=(anywhere, smem),
        scratch_shapes=[
            pltpu.VMEM((lx, ly, lz), F32),
            pltpu.VMEM((lx, ly, lz), jnp.int32),
            pltpu.VMEM((CASES, lx, ly, lz), BF16),
            pltpu.VMEM((lx, ly, lz), F32),
            pltpu.VMEM((per, 2 * CASES * lz), BF16),
            pltpu.VMEM((2 * CASES * lz, 2 * lz), BF16),
            pltpu.VMEM((16, 2 * CASES * lz), BF16),
            pltpu.VMEM((32, lz), BF16),
            pltpu.VMEM((lx + 2 * RADIUS, ly + 2 * YO, lz), F32),
            pltpu.VMEM((XG, ly + 2 * YO, lz), F32),
            pltpu.VMEM((lx, ly, lz), F32),
            pltpu.VMEM((16, lz), F32),
            pltpu.VMEM((n, 16, lz), F32),
            pltpu.VMEM((n, 8, lz), F32),
            pltpu.VMEM((n, 8, lz), F32),
            pltpu.VMEM((n, 8, lz), F32),
            pltpu.VMEM((n, 8, lz), F32),
            pltpu.VMEM((n, 8, lz), F32),
            pltpu.VMEM((8, lz), F32),
            pltpu.VMEM((others, 8, lz), F32),
            pltpu.VMEM((8, lz), F32),
            pltpu.VMEM((n, 8, lz), F32),
            pltpu.VMEM((RADIUS, ly, lz), BF16),
            pltpu.VMEM((RADIUS, ly, lz), BF16),
            pltpu.VMEM((2, RADIUS, lx, lz), BF16),
            pltpu.VMEM((2, RADIUS, lx, lz), BF16),
            pltpu.VMEM((2, RADIUS, RADIUS, lz), BF16),
            pltpu.VMEM((2, RADIUS, RADIUS, lz), BF16),
            dma((3, groups)),
            dma((groups,)),
            dma((n,)),
            dma((n,)),
            dma((n,)),
            dma((n,)),
            dma((n,)),
            dma((n,)),
            dma((others,)),
            dma((others,)),
            dma((n,)),
            dma((n,)),
            dma(()),
            dma(()),
            dma((2,)),
            dma((2,)),
            dma((2,)),
            dma((2,)),
        ],
        compiler_params=pltpu.CompilerParams(
            collective_id=0, has_side_effects=True, vmem_limit_bytes=56 * 1024 * 1024
        ),
        name="sensitivity",
    )(density, design_mask, energy, decay, case_index, case_weight)


def solution(mesh):
    shape = mesh.shape
    n, ngx, ngy = shape["gz"], shape["gx"], shape["gy"]

    def whole(density, design_mask, energy, decay, case_index, case_weight):
        nx, ny, nz = density.shape
        sizes = (n, ngx, ngy, nx // ngx, ny // ngy, nz // n, nx * ny * nz)
        return jax.shard_map(
            functools.partial(local_step, sizes),
            mesh=mesh,
            in_specs=(
                P("gx", "gy", "gz"), P("gx", "gy", "gz"), P(None, "gx", "gy", "gz"), P(None, "gz"), P(), P(),
            ),
            out_specs=(P("gx", "gy", "gz"), P()),
            check_vma=False,
        )(density, design_mask, energy, decay, case_index, case_weight)

    return whole
```

profile of v0, /device:TPU:1, one launch (start us, length us, event | category | flops | bytes accessed | tf_op | source)
XLA Modules:
  0.0 51.1 jit_solution(15642341931256795243)
XLA Ops:
  0.6 46.7 %sensitivity.1 = (f32[64,64,128]{2,1,0:T(8,128)}, f32[4]{0:T(128)}) custom-call(f32[64,64,128]{2,1,0:T(8,128)} %dens_hbm.1, s32[64,64,128]{2,1,0:T(8,128)} %mask_hbm.1, bf16[4,64,64,128]{3,2,1,0:T(8,128)(2,1)} %en_hbm.1, f32[4,128]{1,0:T(4,128)} %decay_ref.1, s32[4]{0:T(128)} %index_ref.1, f32[16]{0:T(128)} %weight_ref.1), custom_call_target="tpu_custom_call" | custom-call | tf_op jit(solution)/shard_map/sensitivity/pallas_call | solution.py:377
  47.4 0.0 copy-start
  47.4 3.2 %copy.10 = f32[64,64,128]{2,1,0:T(8,128)} copy(f32[64,64,128]{2,1,0:T(8,128)} %get-tuple-element.4) | data formatting | bytes 4194304
  50.6 0.0 copy-done
  50.6 0.5 %copy.11 = f32[4]{0:T(128)} copy(f32[4]{0:T(128)S(1)} %copy-done) | data formatting | bytes 32
Async XLA Ops:
  47.4 3.2 %copy-start = (f32[4]{0:T(128)S(1)}, f32[4]{0:T(128)}, u32[]{:S(2)}) copy-start(f32[4]{0:T(128)} %get-tuple-element.5) | copy-start | bytes 52
where the time goes:
time: 51.2 us; the launch traced here: 51.1 us
  Pallas kernels  46.7 us (91%)
  local copies, waits for them, and re-layouts  3.68 us (7%)
  between operations  0.65 us (1%)
    pallas_call x1, Pallas kernels, local_step(): pl.pallas_call(functools.partial(kernel, sizes), out_shape=(jax.ShapeDtyp...  46.7 us
    unnamed x4, local copies, waits for them, and re-layouts  3.68 us

commit v1 on v0

v1 whole, which is shorter than its diff:
```python
import functools
import math

import jax
import jax.numpy as jnp
from jax import lax
from jax.experimental import pallas as pl
from jax.experimental.pallas import tpu as pltpu
from jax.sharding import PartitionSpec as P

CASES = 4
RADIUS = 3
F32 = jnp.float32
BF16 = jnp.bfloat16
MESH = pl.DeviceIdType.MESH
HIGH = lax.Precision.HIGHEST
XG = 8
BATCH = 2
EARLY = 4
YO = 8

_raw = [math.exp(-2.0 * k * k / (RADIUS * RADIUS)) for k in range(-RADIUS, RADIUS + 1)]
TAPS = [t / sum(_raw) for t in _raw]


def dot(a, b, ca, cb, precision=None):
    return lax.dot_general(a, b, (((ca,), (cb,)), ((), ())), precision=precision, preferred_element_type=F32)


def split(value):
    hi = value.astype(BF16)
    return hi, (value - hi.astype(F32)).astype(BF16)


def split_small(value):
    wide = value * 65537.0
    hi = wide - (wide - value)
    return hi.astype(BF16), (value - hi).astype(BF16)


def taps(get):
    acc = TAPS[RADIUS] * get(RADIUS)
    for t in range(RADIUS):
        acc = acc + TAPS[t] * (get(t) + get(2 * RADIUS - t))
    return acc


def kernel(
    sizes, dens_hbm, mask_hbm, en_hbm, decay_ref, index_ref, weight_ref,
    fm, scale, fc, vmap, comp_out,
    dens, mask, en, lhs, maps, coef, ext, tmp,
    consts_out, consts_in, fh_out, fh_in, fin, carry_out, cx, yf, yr,
    cs_out, cs_in, ct_out, ct_in, xs_out, xs_in, ys_out, ys_in, ds_out, ds_in, st_out, st_in, st_sum,
    load_sem, cst_s, cst_r, ph1_s, ph1_r, ph2_s, ph2_r, cs_s, cs_r, ct_s, ct_r,
    xs_s, xs_r, ys_s, ys_r, ds_s, ds_r, cb_s, cb_r, st_s, st_r, dg_s, dg_r,
):
    n, ngx, ngy, lx, ly, lz, cells = sizes
    groups = lx // XG
    per = XG * ly
    blocks = per // lz
    gz, gx, gy = lax.axis_index("gz"), lax.axis_index("gx"), lax.axis_index("gy")
    others = ngx * ngy - 1
    mine = gz // blocks

    def peer(k):
        flat = lax.rem(gx * ngy + gy + 1 + k, ngx * ngy)
        return {"gz": gz, "gx": flat // ngy, "gy": lax.rem(flat, ngy)}

    def group_at(i):
        j = (i + 1) // 2
        off = jnp.where(lax.rem(i, 2) == 1, groups // 2 - j, groups // 2 + j)
        return lax.rem(mine + off, groups)

    def each_far(body):
        for k in sorted(range(1, n), key=lambda k: -min(k // blocks, (n - k) // blocks)):
            body(jnp.where(gz + k >= n, gz + k - n, gz + k))

    def end(ref, sem):
        pltpu.make_async_copy(ref, ref, sem).wait()

    def loads(k):
        rows = pl.ds(k * XG, XG)
        return (
            pltpu.make_async_copy(dens_hbm.at[rows], dens.at[rows], load_sem.at[0, k]),
            pltpu.make_async_copy(mask_hbm.at[rows], mask.at[rows], load_sem.at[1, k]),
            pltpu.make_async_copy(en_hbm.at[:, rows], en.at[:, rows], load_sem.at[2, k]),
        )

    def start_loads(i, _):
        for copy in loads(group_at(i)):
            copy.start()
        return 0

    lax.fori_loop(0, groups, start_loads, 0)

    for i in (0, 1, n + 2, n + 3):
        cx[i] = jnp.zeros((8, lz), F32)
    st_in[...] = jnp.zeros_like(st_in)

    barrier = pltpu.get_barrier_semaphore()

    def greet(k, _):
        pl.semaphore_signal(barrier, inc=1, device_id={"gz": lax.rem(gz + k, n)}, device_id_type=MESH)
        return 0

    lax.fori_loop(1, n, greet, 0)
    for k in range(others):
        pl.semaphore_signal(barrier, inc=1, device_id=peer(k), device_id_type=MESH)

    decay = jnp.concatenate([decay_ref[...], decay_ref[...]], axis=0)
    logs = jnp.log(decay)
    row = lax.broadcasted_iota(jnp.int32, (lz, lz), 0)
    col = lax.broadcasted_iota(jnp.int32, (lz, lz), 1)
    low, high = row <= col, row >= col
    up = dot(logs, low.astype(F32), 1, 0, HIGH)
    down = dot(logs, high.astype(F32), 1, 0, HIGH)
    keep = 1.0 - decay
    columns = jnp.transpose(jnp.concatenate([up, down, keep, keep], axis=0))
    total = up[:, lz - 1 : lz]
    fwd_last = jnp.exp(total - up) * keep
    first = jnp.exp(down[:, 0:1] - down) * keep
    lead = jnp.exp(up)
    trail = jnp.exp(down)
    rows8 = lax.broadcasted_iota(jnp.int32, (8, lz), 0)
    rows16 = lax.broadcasted_iota(jnp.int32, (16, lz), 0)
    lane = lax.broadcasted_iota(jnp.int32, (8, lz), 1)
    couple = jnp.sum(first * lead, axis=1, keepdims=True)
    consts_out[...] = jnp.where(rows8 < CASES, jnp.exp(total), couple)
    consts_in[gz] = consts_out[...]

    vals = jnp.zeros((8, lz), F32)
    for c in range(CASES):
        wc = weight_ref[index_ref[c]] * -3.0
        up_col, down_col, keep_col = columns[:, c : c + 1], columns[:, 8 + c : 9 + c], columns[:, 16 + c : 17 + c]
        fwd_t = jnp.where(low, jnp.exp(jnp.where(low, up[c : c + 1] - up_col, 0.0)), 0.0) * keep_col
        bwd_t = jnp.where(high, jnp.exp(jnp.where(high, down[c : c + 1] - down_col, 0.0)), 0.0) * keep_col
        both = dot(fwd_t, bwd_t, 1, 0, HIGH) * wc
        hi, lo = split(both)
        for half in range(2):
            at = (2 * c + half) * lz
            maps[at : at + lz, 0:lz] = hi
            maps[at : at + lz, lz : 2 * lz] = lo
        hrow = dot(first, fwd_t, 1, 1, HIGH)
        lead_map = dot(lead, bwd_t, 1, 0, HIGH)
        cblock = jnp.where(rows8 == c, fwd_last, 0.0)
        cblock = jnp.where(rows8 == c + CASES, hrow, cblock)
        chi = cblock.astype(BF16).astype(F32)
        pair = jnp.concatenate([chi, cblock - chi], axis=0).astype(BF16)
        for half in range(2):
            at = (2 * c + half) * lz
            coef[0:16, at : at + lz] = pair
            coef[16:32, at : at + lz] = (rows16 == c).astype(F32).astype(BF16)
        vals = jnp.where(rows8 == c, lead_map * wc, vals)
        vals = jnp.where(rows8 == c + CASES, trail * wc, vals)
    vhi = vals.astype(BF16).astype(F32)
    vmap[...] = jnp.concatenate([vhi, vhi, vals - vhi, jnp.zeros((8, lz), F32)], axis=0).astype(BF16)

    def local(at, sums):
        k = group_at(at)
        for copy in loads(k):
            copy.wait()
        for i in range(XG):
            x = k * XG + i
            d, m = dens[x], mask[x]
            dense = jnp.where(m == 1, 0.001, jnp.where(m == 2, 1.0, d))
            cube = dense * dense * dense
            for c in range(CASES):
                hi, lo = split_small(cube * en[c, x].astype(F32))
                lhs[k, i * ly : (i + 1) * ly, 2 * c * lz : (2 * c + 1) * lz] = hi
                lhs[k, i * ly : (i + 1) * ly, (2 * c + 1) * lz : (2 * c + 2) * lz] = lo
        fh = dot(coef[...], lhs[k], 1, 1)
        for b in range(blocks):
            piece = fh[:, b * lz : (b + 1) * lz]
            fh_out[k * blocks + b] = piece[0:8] + piece[8:16]
            sums = sums + piece[16:24]
        return sums

    def to_slab(src, dst, send, recv, k):
        return pltpu.make_async_remote_copy(
            src_ref=src, dst_ref=dst, send_sem=send, recv_sem=recv,
            device_id={"gz": k}, device_id_type=MESH,
        )

    def consts_copy(src, dst):
        return to_slab(consts_out, consts_in.at[src], cst_s, cst_r, dst)

    def ph1_copy(src, dst):
        return to_slab(fh_out.at[dst], fh_in.at[src], ph1_s, ph1_r, dst)

    def ph2_copy(src, dst):
        return to_slab(carry_out.at[dst], cx.at[2 + src], ph2_s, ph2_r, dst)

    def ct_copy(src, dst):
        return to_slab(ct_out, ct_in.at[src], ct_s, ct_r, dst)

    def send_group(at):
        for b in range(blocks):
            p = group_at(at) * blocks + b

            @pl.when(p != gz)
            def _():
                ph1_copy(gz, p).start()

    sums = lax.fori_loop(0, EARLY, local, jnp.zeros((8, lz), F32))
    pl.semaphore_wait(barrier, n - 1 + others)
    for at in range(EARLY):
        send_group(at)
    each_far(lambda p: consts_copy(gz, p).start())

    def local_send(at, sums):
        sums = local(at, sums)
        send_group(at)
        return sums

    sums = lax.fori_loop(EARLY, groups, local_send, sums)
    fh_in[gz] = fh_out[gz]

    sums = jnp.sum(sums, axis=1, keepdims=True)
    part = jnp.sum(jnp.where(rows8 == lane, sums, 0.0), axis=0, keepdims=True)
    cs_out[...] = part

    def cs_copy(k):
        return pltpu.make_async_remote_copy(
            src_ref=cs_out, dst_ref=cs_in.at[k], send_sem=cs_s.at[k], recv_sem=cs_r.at[k],
            device_id=peer(k), device_id_type=MESH,
        )

    for k in range(others):
        cs_copy(k).start()

    for j in range(RADIUS):
        ext[j] = jnp.zeros((ly + 2 * YO, lz), F32)
        ext[RADIUS + lx + j] = jnp.zeros((ly + 2 * YO, lz), F32)
    ext[:, 0:YO] = jnp.zeros((lx + 2 * RADIUS, YO, lz), F32)
    ext[:, YO + ly :] = jnp.zeros((lx + 2 * RADIUS, YO, lz), F32)

    def smoothed(k, _):
        full = dot(lhs[k], maps[...], 1, 0)
        full = full[:, :lz] + full[:, lz:]
        ext[pl.ds(RADIUS + k * XG, XG), YO : YO + ly, :] = full.reshape(XG, ly, lz)
        for i in range(XG):
            x = k * XG + i
            scale[x] = jnp.where(mask[x] == 0, 1.0 / jnp.maximum(dens[x], 0.1), 0.0)
        return 0

    lax.fori_loop(0, groups, smoothed, 0)

    xs_at = jnp.where(gx == 0, lx - RADIUS, 0)
    for j in range(RADIUS):
        xs_out[j] = ext[RADIUS + xs_at + j, YO : YO + ly, :].astype(BF16)
    for side in range(2):
        for j in range(RADIUS):
            y = YO + (j if side == 0 else ly - RADIUS + j)
            ys_out[side, j] = ext[RADIUS : RADIUS + lx, y, :].astype(BF16)
            ds_out[side, j] = ext[pl.ds(RADIUS + xs_at, RADIUS), y, :].astype(BF16)

    def beside(src, dst, send, recv, where):
        return pltpu.make_async_remote_copy(
            src_ref=src, dst_ref=dst, send_sem=send, recv_sem=recv, device_id=where, device_id_type=MESH
        )

    def x_copy():
        return beside(xs_out, xs_in, xs_s, xs_r, {"gx": 1 - gx})

    def y_copy(side, to):
        return beside(ys_out.at[side], ys_in.at[1 - side], ys_s.at[side], ys_r.at[1 - side], {"gy": to})

    def d_copy(side, to):
        where = {"gx": 1 - gx, "gy": to}
        return beside(ds_out.at[side], ds_in.at[1 - side], ds_s.at[side], ds_r.at[1 - side], where)

    def blocks_copy():
        src = jnp.where(gx == 0, n, 2)
        dst = jnp.where(gx == 0, 0, n + 2)
        return beside(cx.at[pl.ds(src, 2)], cx.at[pl.ds(dst, 2)], cb_s, cb_r, {"gx": 1 - gx})

    def blocks_arrive():
        dst = jnp.where(gx == 0, n + 2, 0)
        return beside(cx.at[pl.ds(dst, 2)], cx.at[pl.ds(dst, 2)], cb_s, cb_r, {"gx": 1 - gx})

    def strip_copy(side, to):
        where = {"gy": to}
        return beside(st_out.at[side], st_in.at[1 - side, 1:3], st_s.at[side], st_r.at[1 - side], where)

    def corner_copy(side, to):
        where = {"gx": 1 - gx, "gy": to}
        dst = st_in.at[1 - side, jnp.where(gx == 0, 0, 3)]
        return beside(st_out.at[side, 1 - gx], dst, dg_s.at[side], dg_r.at[1 - side], where)

    def corner_arrive(side, to):
        where = {"gx": 1 - gx, "gy": to}
        dst = st_in.at[side, jnp.where(gx == 0, 3, 0)]
        return beside(st_out.at[side, 1 - gx], dst, dg_s.at[side], dg_r.at[side], where)

    def sides(body):
        @pl.when(gy > 0)
        def _():
            body(0, gy - 1)

        @pl.when(gy < ngy - 1)
        def _():
            body(1, gy + 1)

    x_copy().start()

    def send_halo(side, to):
        y_copy(side, to).start()
        d_copy(side, to).start()

    sides(send_halo)

    def gains(s):
        both = consts_in[s]
        turned = pltpu.roll(both, CASES, 0)
        return jnp.where(rows8 < CASES, both, turned), jnp.where(rows8 < CASES, turned, both)

    def ascend(s, state):
        fin[s] = state
        return gains(s)[0] * state + fh_in[s]

    end(fh_in.at[0 : n - 1], cst_r)
    end(fh_in.at[0 : n - 1], ph1_r)
    lax.fori_loop(0, n, ascend, jnp.zeros((8, lz), F32))

    def descend(k, state):
        s = n - 1 - k
        entering = fin[s]
        carry_out[s] = jnp.where(rows8 < CASES, entering, state)
        gain, mix = gains(s)
        return gain * state + fh_in[s] + mix * pltpu.roll(entering, CASES, 0)

    lax.fori_loop(0, n, descend, jnp.zeros((8, lz), F32))
    each_far(lambda p: ph2_copy(gz, p).start())
    cx[2 + gz] = carry_out[gz]
    for k in range(others):
        cs_copy(k).wait_recv()
        part = part + cs_in[k]
    ct_out[...] = part
    ct_in[gz] = part
    each_far(lambda p: ct_copy(gz, p).start())


    halo_x = jnp.where(gx == 0, RADIUS + lx, 0)
    x_copy().wait()
    ext[pl.ds(halo_x, RADIUS), YO : YO + ly, :] = xs_in[...].astype(F32)

    def take(side, to):
        for copy in (y_copy, d_copy):
            copy(side, to).wait_send()
            copy(1 - side, to).wait_recv()
        for j in range(RADIUS):
            y = YO + (j - RADIUS if side == 0 else ly + j)
            ext[RADIUS : RADIUS + lx, y, :] = ys_in[side, j].astype(F32)
            ext[pl.ds(halo_x, RADIUS), y, :] = ds_in[side, j].astype(F32)

    sides(take)

    def filtered(k, _):
        for i in range(XG):
            x = k * XG + i
            tmp[i] = taps(lambda t: ext[x + t])
            fm[x] = taps(lambda t: tmp[i, YO - RADIUS + t : YO - RADIUS + t + ly, :])
        return 0

    lax.fori_loop(0, groups, filtered, 0)

    end(fh_in.at[0 : n - 1], ph2_r)
    blocks_copy().start()
    half_y = lax.rem(lane, ly)
    slot = half_y // 4
    for side in range(2):
        y0 = 0 if side == 0 else ly - RADIUS
        for half in range(2):
            packed = jnp.zeros((8, lz), F32)
            for q in range(n // 2):
                moved = pltpu.roll(cx[2 + half * (n // 2) + q], (4 * q - y0) % lz, 1)
                packed = jnp.where(slot == q, moved, packed)
            st_out[side, half] = packed

    def send_strip(side, to):
        strip_copy(side, to).start()
        corner_copy(side, to).start()

    sides(send_strip)
    def add_ct(s, state):
        return state + ct_in[s]

    end(ct_in.at[0 : n - 1], ct_r)
    comp_out[...] = lax.fori_loop(0, n, add_ct, jnp.zeros((1, lz), F32)) * (1.0 / cells)

    for sem in (cst_s, ph1_s, ph2_s):
        end(fh_in.at[0 : n - 1], sem)
    end(ct_in.at[0 : n - 1], ct_s)
    for k in range(others):
        cs_copy(k).wait_send()

    def along_y(k, _):
        for b in range(4):
            i = k * 4 + b
            state = cx[2 + i]
            acc = TAPS[RADIUS] * state
            for t in range(1, RADIUS + 1):
                down_y = jnp.where(half_y >= t, pltpu.roll(state, t, 1), 0.0)
                up_y = jnp.where(half_y < ly - t, pltpu.roll(state, lz - t, 1), 0.0)
                acc = acc + TAPS[RADIUS + t] * (down_y + up_y)
            yf[2 + i] = acc
        return 0

    lax.fori_loop(0, n // 4, along_y, 0)

    blocks_copy().wait_send()
    blocks_arrive().wait_recv()
    for i in (0, 1, n + 2, n + 3):
        state = cx[i]
        acc = TAPS[RADIUS] * state
        for t in range(1, RADIUS + 1):
            down_y = jnp.where(half_y >= t, pltpu.roll(state, t, 1), 0.0)
            up_y = jnp.where(half_y < ly - t, pltpu.roll(state, lz - t, 1), 0.0)
            acc = acc + TAPS[RADIUS + t] * (down_y + up_y)
        yf[i] = acc

    def take_strip(side, to):
        strip_copy(side, to).wait_send()
        corner_copy(side, to).wait_send()
        strip_copy(1 - side, to).wait_recv()
        corner_arrive(side, to).wait_recv()

    sides(take_strip)

    for side in range(2):
        for quarter in range(4):
            strip = st_in[side, quarter]
            total_y = jnp.zeros((8, lz), F32)
            for y in range(RADIUS):
                for j in range(RADIUS):
                    far = y + j + 1
                    if far > RADIUS:
                        continue
                    at = RADIUS - 1 - j if side == 0 else j
                    to = y if side == 0 else RADIUS - 1 - y
                    moved = strip if at == to else pltpu.roll(strip, (to - at) % lz, 1)
                    total_y = total_y + jnp.where(lax.rem(lane, 4) == to, TAPS[RADIUS + far] * moved, 0.0)
            st_sum[side, quarter] = total_y

    def add_strips(k, _):
        for b in range(4):
            i = k * 4 + b
            at = i + n // 2 - 2
            quarter, q = at // (n // 2), lax.rem(at, n // 2)
            mine_y = slot == q
            low_y = pltpu.roll(jnp.where(mine_y, st_sum[0, quarter], 0.0), lz - 4 * q, 1)
            high_y = pltpu.roll(jnp.where(mine_y, st_sum[1, quarter], 0.0), lz + ly - RADIUS - 4 * q, 1)
            acc = yf[i] + low_y + high_y
            yf[i] = acc
            yr[i] = pltpu.roll(acc, ly, 1)
        return 0

    lax.fori_loop(0, (n + 4) // 4, add_strips, 0)
    first_half = lane < ly

    def along_x(k, _):
        for b in range(4):
            p = k * 4 + b
            i = p + 2
            near = yr[i] + jnp.where(first_half, yr[i - 1], yr[i + 1])
            far = jnp.where(first_half, yr[i - 2] + yr[i + 1], yr[i - 1] + yr[i + 2])
            acc = TAPS[RADIUS] * yf[i] + TAPS[RADIUS + 1] * near
            fc[p] = acc + TAPS[RADIUS + 2] * (yf[i - 1] + yf[i + 1]) + TAPS[RADIUS + 3] * far
        return 0

    lax.fori_loop(0, n // 4, along_x, 0)


def last(fm, scale, fc, vmap, comp_in, out_hbm, comp_out, out, sem):
    lx, ly, lz = fm.shape
    rows_per = lz // ly
    n = fc.shape[0]
    step = 4
    for c in range(CASES):
        comp_out[c] = jnp.sum(comp_in[0:1, c : c + 1])

    def out_copy(k):
        rows = pl.ds(k * step * rows_per, step * rows_per)
        return pltpu.make_async_copy(out.at[rows], out_hbm.at[rows], sem.at[k])

    def finish(t, _):
        for b in range(BATCH * step):
            p = t * BATCH * step + b
            state = fc[p]
            hi = state.astype(BF16).astype(F32)
            stack = jnp.concatenate([hi, state - hi, hi, jnp.zeros((8, lz), F32)], axis=0)
            add = dot(jnp.transpose(stack).astype(BF16), vmap[...], 1, 0).reshape(rows_per, ly, lz)
            at = pl.ds(p * rows_per, rows_per)
            out[at] = (fm[at] + add) * scale[at]
        for b in range(BATCH):
            out_copy(t * BATCH + b).start()
        return 0

    lax.fori_loop(0, n // (BATCH * step), finish, 0)

    def drain_out(k, _):
        out_copy(k).wait()
        return 0

    lax.fori_loop(0, n // step, drain_out, 0)


def local_step(sizes, density, design_mask, energy, decay, case_index, case_weight):
    n, ngx, ngy, lx, ly, lz, cells = sizes
    groups = lx // XG
    per = XG * ly
    others = ngx * ngy - 1
    dma = pltpu.SemaphoreType.DMA
    anywhere = pl.BlockSpec(memory_space=pltpu.HBM)
    smem = pl.BlockSpec(memory_space=pltpu.SMEM)
    vmem = pl.BlockSpec(memory_space=pltpu.VMEM)
    state = pltpu.VMEM((n, 8, lz), F32)
    fm, scale, fc, vmap, comp = pl.pallas_call(
        functools.partial(kernel, sizes),
        out_shape=(
            jax.ShapeDtypeStruct((lx, ly, lz), F32),
            jax.ShapeDtypeStruct((lx, ly, lz), F32),
            jax.ShapeDtypeStruct((n, 8, lz), F32),
            jax.ShapeDtypeStruct((32, lz), BF16),
            jax.ShapeDtypeStruct((1, lz), F32),
        ),
        in_specs=[anywhere, anywhere, anywhere, vmem, smem, smem],
        out_specs=(vmem,) * 5,
        scratch_shapes=[
            pltpu.VMEM((lx, ly, lz), F32),
            pltpu.VMEM((lx, ly, lz), jnp.int32),
            pltpu.VMEM((CASES, lx, ly, lz), BF16),
            pltpu.VMEM((groups, per, 2 * CASES * lz), BF16),
            pltpu.VMEM((2 * CASES * lz, 2 * lz), BF16),
            pltpu.VMEM((32, 2 * CASES * lz), BF16),
            pltpu.VMEM((lx + 2 * RADIUS, ly + 2 * YO, lz), F32),
            pltpu.VMEM((XG, ly + 2 * YO, lz), F32),
            pltpu.VMEM((8, lz), F32),
            state,
            state,
            state,
            state,
            state,
            pltpu.VMEM((n + 4, 8, lz), F32),
            pltpu.VMEM((n + 4, 8, lz), F32),
            pltpu.VMEM((n + 4, 8, lz), F32),
            pltpu.VMEM((1, lz), F32),
            pltpu.VMEM((others, 1, lz), F32),
            pltpu.VMEM((1, lz), F32),
            pltpu.VMEM((n, 1, lz), F32),
            pltpu.VMEM((RADIUS, ly, lz), BF16),
            pltpu.VMEM((RADIUS, ly, lz), BF16),
            pltpu.VMEM((2, RADIUS, lx, lz), BF16),
            pltpu.VMEM((2, RADIUS, lx, lz), BF16),
            pltpu.VMEM((2, RADIUS, RADIUS, lz), BF16),
            pltpu.VMEM((2, RADIUS, RADIUS, lz), BF16),
            pltpu.VMEM((2, 2, 8, lz), F32),
            pltpu.VMEM((2, 4, 8, lz), F32),
            pltpu.VMEM((2, 4, 8, lz), F32),
            dma((3, groups)),
            dma(()),
            dma(()),
            dma(()),
            dma(()),
            dma(()),
            dma(()),
            dma((others,)),
            dma((others,)),
            dma(()),
            dma(()),
            dma(()),
            dma(()),
            dma((2,)),
            dma((2,)),
            dma((2,)),
            dma((2,)),
            dma(()),
            dma(()),
            dma((2,)),
            dma((2,)),
            dma((2,)),
            dma((2,)),
        ],
        compiler_params=pltpu.CompilerParams(
            collective_id=0, has_side_effects=True, vmem_limit_bytes=40 * 1024 * 1024
        ),
        name="states",
    )(*(pltpu.with_memory_space_constraint(v, pltpu.HBM) for v in (density, design_mask, energy, decay, case_index, case_weight)))
    return pl.pallas_call(
        last,
        out_shape=(
            jax.ShapeDtypeStruct((lx, ly, lz), F32),
            jax.ShapeDtypeStruct((CASES,), F32),
        ),
        in_specs=[vmem] * 5,
        out_specs=(anywhere, smem),
        scratch_shapes=[pltpu.VMEM((lx, ly, lz), F32), dma((n // 4,))],
        compiler_params=pltpu.CompilerParams(vmem_limit_bytes=20 * 1024 * 1024),
        name="result",
    )(fm, scale, fc, vmap, comp)


def solution(mesh):
    shape = mesh.shape
    n, ngx, ngy = shape["gz"], shape["gx"], shape["gy"]

    def whole(density, design_mask, energy, decay, case_index, case_weight):
        nx, ny, nz = density.shape
        sizes = (n, ngx, ngy, nx // ngx, ny // ngy, nz // n, nx * ny * nz)
        return jax.shard_map(
            functools.partial(local_step, sizes),
            mesh=mesh,
            in_specs=(
                P("gx", "gy", "gz"), P("gx", "gy", "gz"), P(None, "gx", "gy", "gz"), P(None, "gz"), P(), P(),
            ),
            out_specs=(P("gx", "gy", "gz"), P()),
            check_vma=False,
        )(density, design_mask, energy, decay, case_index, case_weight)

    return whole
```

time: 51.2 us -> 36.7 us (0.72)
  Pallas kernels: 46.7 us -> 35.9 us
  local copies, waits for them, and re-layouts: 3.68 us -> 0 us
    pallas_call x1, Pallas kernels: 46.7 us -> 33.3 us  [local_step(): pl.pallas_call(functools.partial(kernel, sizes), out_shape=(jax.ShapeDtyp...]
    unnamed x4 -> x0, local copies, waits for them, and re-layouts: 3.68 us -> none
    pallas_call x0 -> x1, Pallas kernels: none -> 2.67 us  [local_step(): pl.pallas_call(last, out_shape=(jax.ShapeDtypeStruct((lx, ly, lz), F32),...]
where the time goes in v1:
time: 36.7 us; the launch traced here: 36.6 us
  Pallas kernels  35.9 us (98%)
  between operations  0.64 us (2%)
    pallas_call x1, Pallas kernels, local_step(): pl.pallas_call(functools.partial(kernel, sizes), out_shape=(jax.ShapeDtyp...  33.3 us
    pallas_call x1, Pallas kernels, local_step(): pl.pallas_call(last, out_shape=(jax.ShapeDtypeStruct((lx, ly, lz), F32),...  2.67 us

profile of v1, /device:TPU:1, one launch (start us, length us, event | category | flops | bytes accessed | tf_op | source)
XLA Modules:
  0.0 36.6 jit_solution(12651410335994186344)
XLA Ops:
  0.6 33.3 %states.1 = (f32[64,64,128]{2,1,0:T(8,128)S(1)}, f32[64,64,128]{2,1,0:T(8,128)S(1)}, f32[32,8,128]{2,1,0:T(8,128)S(1)}, bf16[32,128]{1,0:T(8,128)(2,1)S(1)}, f32[1,128]{1,0:T(1,128)S(1)}) custom-call(f32[64,64,128]{2,1,0:T(8,128)} %dens_hbm.1, s32[64,64,128]{2,1,0:T(8,128)} %mask_hbm.1, bf16[4,64,64,128]{3,2,1,0:T(8,128)(2,1)} %en_hbm.1, ...), custom_call_target="tpu_custom_call" | custom-call | tf_op jit(solution)/shard_map/states/pallas_call | solution.py:518
  33.9 2.7 %result.1 = (f32[64,64,128]{2,1,0:T(8,128)}, f32[4]{0:T(128)}) custom-call(f32[64,64,128]{2,1,0:T(8,128)S(1)} %get-tuple-element.7.fm, f32[64,64,128]{2,1,0:T(8,128)S(1)} %get-tuple-element.8.scale, f32[32,8,128]{2,1,0:T(8,128)S(1)} %get-tuple-element.9.fc, bf16[32,128]{1,0:T(8,128)(2,1)S(1)} %get-tuple-element.10.vmap, f32[1,128]{1,0:T(1,128)S(1)} %get-tuple-element.11.comp_in), custom_call_target="tpu_custom_call" | custom-call | tf_op jit(solution)/shard_map/result/pallas_call | solution.py:589

commit v2 on v1

--- a/solution.py
+++ b/solution.py
@@ -15,7 +15,8 @@
 MESH = pl.DeviceIdType.MESH
 HIGH = lax.Precision.HIGHEST
 XG = 8
-BATCH = 2
+BATCH = 8
+PIECES = 8
 EARLY = 4
 YO = 8
 
@@ -30,12 +31,6 @@
 def split(value):
     hi = value.astype(BF16)
     return hi, (value - hi.astype(F32)).astype(BF16)
-
-
-def split_small(value):
-    wide = value * 65537.0
-    hi = wide - (wide - value)
-    return hi.astype(BF16), (value - hi).astype(BF16)
 
 
 def taps(get):
@@ -47,9 +42,9 @@
 
 def kernel(
     sizes, dens_hbm, mask_hbm, en_hbm, decay_ref, index_ref, weight_ref,
-    fm, scale, fc, vmap, comp_out,
-    dens, mask, en, lhs, maps, coef, ext, tmp,
-    consts_out, consts_in, fh_out, fh_in, fin, carry_out, cx, yf, yr,
+    fm, comp_out,
+    dens, mask, en, fwd, lhs, maps, coef, ext, tmp, scale, fc, vmap, inv, cf,
+    consts_out, consts_in, gain, mix, fh_out, fh_in, fin, carry_out, cx, yf, yr,
     cs_out, cs_in, ct_out, ct_in, xs_out, xs_in, ys_out, ys_in, ds_out, ds_in, st_out, st_in, st_sum,
     load_sem, cst_s, cst_r, ph1_s, ph1_r, ph2_s, ph2_r, cs_s, cs_r, ct_s, ct_r,
     xs_s, xs_r, ys_s, ys_r, ds_s, ds_r, cb_s, cb_r, st_s, st_r, dg_s, dg_r,
@@ -78,6 +73,10 @@
     def end(ref, sem):
         pltpu.make_async_copy(ref, ref, sem).wait()
 
+    for i in (0, 1, n + 2, n + 3):
+        cx[i] = jnp.zeros((8, lz), BF16)
+    st_in[...] = jnp.zeros_like(st_in)
+
     def loads(k):
         rows = pl.ds(k * XG, XG)
         return (
@@ -91,21 +90,12 @@
             copy.start()
         return 0
 
-    lax.fori_loop(0, groups, start_loads, 0)
-
-    for i in (0, 1, n + 2, n + 3):
-        cx[i] = jnp.zeros((8, lz), F32)
-    st_in[...] = jnp.zeros_like(st_in)
-
+    lax.fori_loop(0, 2, start_loads, 0)
     barrier = pltpu.get_barrier_semaphore()
-
-    def greet(k, _):
-        pl.semaphore_signal(barrier, inc=1, device_id={"gz": lax.rem(gz + k, n)}, device_id_type=MESH)
-        return 0
-
-    lax.fori_loop(1, n, greet, 0)
+    each_far(lambda p: pl.semaphore_signal(barrier, inc=1, device_id={"gz": p}, device_id_type=MESH))
     for k in range(others):
         pl.semaphore_signal(barrier, inc=1, device_id=peer(k), device_id_type=MESH)
+    lax.fori_loop(2, groups, start_loads, 0)
 
     decay = jnp.concatenate([decay_ref[...], decay_ref[...]], axis=0)
     logs = jnp.log(decay)
@@ -125,23 +115,15 @@
     rows16 = lax.broadcasted_iota(jnp.int32, (16, lz), 0)
     lane = lax.broadcasted_iota(jnp.int32, (8, lz), 1)
     couple = jnp.sum(first * lead, axis=1, keepdims=True)
-    consts_out[...] = jnp.where(rows8 < CASES, jnp.exp(total), couple)
+    across = jnp.where(rows8 == lane, jnp.exp(total), jnp.where(rows8 + 8 == lane, couple, 0.0))
+    consts_out[...] = jnp.sum(across, axis=0, keepdims=True)
     consts_in[gz] = consts_out[...]
 
-    vals = jnp.zeros((8, lz), F32)
     for c in range(CASES):
-        wc = weight_ref[index_ref[c]] * -3.0
-        up_col, down_col, keep_col = columns[:, c : c + 1], columns[:, 8 + c : 9 + c], columns[:, 16 + c : 17 + c]
-        fwd_t = jnp.where(low, jnp.exp(jnp.where(low, up[c : c + 1] - up_col, 0.0)), 0.0) * keep_col
-        bwd_t = jnp.where(high, jnp.exp(jnp.where(high, down[c : c + 1] - down_col, 0.0)), 0.0) * keep_col
-        both = dot(fwd_t, bwd_t, 1, 0, HIGH) * wc
-        hi, lo = split(both)
-        for half in range(2):
-            at = (2 * c + half) * lz
-            maps[at : at + lz, 0:lz] = hi
-            maps[at : at + lz, lz : 2 * lz] = lo
+        fwd_t = jnp.where(low, jnp.exp(jnp.where(low, up[c : c + 1] - columns[:, c : c + 1], 0.0)), 0.0)
+        fwd_t = fwd_t * columns[:, 16 + c : 17 + c]
+        fwd[c] = fwd_t
         hrow = dot(first, fwd_t, 1, 1, HIGH)
-        lead_map = dot(lead, bwd_t, 1, 0, HIGH)
         cblock = jnp.where(rows8 == c, fwd_last, 0.0)
         cblock = jnp.where(rows8 == c + CASES, hrow, cblock)
         chi = cblock.astype(BF16).astype(F32)
@@ -150,10 +132,15 @@
             at = (2 * c + half) * lz
             coef[0:16, at : at + lz] = pair
             coef[16:32, at : at + lz] = (rows16 == c).astype(F32).astype(BF16)
-        vals = jnp.where(rows8 == c, lead_map * wc, vals)
-        vals = jnp.where(rows8 == c + CASES, trail * wc, vals)
-    vhi = vals.astype(BF16).astype(F32)
-    vmap[...] = jnp.concatenate([vhi, vhi, vals - vhi, jnp.zeros((8, lz), F32)], axis=0).astype(BF16)
+
+    spots = lane.astype(F32) * 0.6180339887 + rows8.astype(F32) * 0.3247179572
+
+    def stretch(p):
+        phase = spots + jnp.asarray(p, jnp.int32).astype(F32) * 0.7548776662
+        return 1.0 + (phase - jnp.floor(phase))
+
+    def operand(k):
+        return jnp.concatenate([lhs[k, c] for c in range(2 * CASES)], axis=1)
 
     def local(at, sums):
         k = group_at(at)
@@ -165,13 +152,13 @@
             dense = jnp.where(m == 1, 0.001, jnp.where(m == 2, 1.0, d))
             cube = dense * dense * dense
             for c in range(CASES):
-                hi, lo = split_small(cube * en[c, x].astype(F32))
-                lhs[k, i * ly : (i + 1) * ly, 2 * c * lz : (2 * c + 1) * lz] = hi
-                lhs[k, i * ly : (i + 1) * ly, (2 * c + 1) * lz : (2 * c + 2) * lz] = lo
-        fh = dot(coef[...], lhs[k], 1, 1)
+                hi, lo = split(cube * en[c, x].astype(F32))
+                lhs[k, 2 * c, i * ly : (i + 1) * ly] = hi
+                lhs[k, 2 * c + 1, i * ly : (i + 1) * ly] = lo
+        fh = dot(coef[...], operand(k), 1, 1)
         for b in range(blocks):
             piece = fh[:, b * lz : (b + 1) * lz]
-            fh_out[k * blocks + b] = piece[0:8] + piece[8:16]
+            fh_out[k * blocks + b] = ((piece[0:8] + piece[8:16]) * stretch(k * blocks + b)).astype(BF16)
             sums = sums + piece[16:24]
         return sums
 
@@ -228,6 +215,22 @@
     for k in range(others):
         cs_copy(k).start()
 
+    vals = jnp.zeros((8, lz), F32)
+    for c in range(CASES):
+        wc = weight_ref[index_ref[c]] * -3.0
+        bwd_t = jnp.where(high, jnp.exp(jnp.where(high, down[c : c + 1] - columns[:, 8 + c : 9 + c], 0.0)), 0.0)
+        bwd_t = bwd_t * columns[:, 16 + c : 17 + c]
+        hi, lo = split(dot(fwd[c], bwd_t, 1, 0, HIGH) * wc)
+        for half in range(2):
+            at = (2 * c + half) * lz
+            maps[at : at + lz, 0:lz] = hi
+            maps[at : at + lz, lz : 2 * lz] = lo
+        lead_map = dot(lead, bwd_t, 1, 0, HIGH)
+        vals = jnp.where(rows8 == c, lead_map * wc, vals)
+        vals = jnp.where(rows8 == c + CASES, trail * wc, vals)
+    vhi = vals.astype(BF16).astype(F32)
+    vmap[...] = jnp.concatenate([vhi, vhi, vals - vhi, jnp.zeros((8, lz), F32)], axis=0).astype(BF16)
+
     for j in range(RADIUS):
         ext[j] = jnp.zeros((ly + 2 * YO, lz), F32)
         ext[RADIUS + lx + j] = jnp.zeros((ly + 2 * YO, lz), F32)
@@ -235,7 +238,7 @@
     ext[:, YO + ly :] = jnp.zeros((lx + 2 * RADIUS, YO, lz), F32)
 
     def smoothed(k, _):
-        full = dot(lhs[k], maps[...], 1, 0)
+        full = dot(operand(k), maps[...], 1, 0)
         full = full[:, :lz] + full[:, lz:]
         ext[pl.ds(RADIUS + k * XG, XG), YO : YO + ly, :] = full.reshape(XG, ly, lz)
         for i in range(XG):
@@ -309,27 +312,24 @@
 
     sides(send_halo)
 
-    def gains(s):
-        both = consts_in[s]
-        turned = pltpu.roll(both, CASES, 0)
-        return jnp.where(rows8 < CASES, both, turned), jnp.where(rows8 < CASES, turned, both)
-
-    def ascend(s, state):
+    for p in range(n):
+        inv[p] = 1.0 / stretch(p)
+    end(ct_in.at[0 : n - 1], cst_r)
+    spread = jnp.transpose(jnp.concatenate([consts_in[s] for s in range(n)], axis=0))
+    for s in range(n):
+        gain[s] = jnp.broadcast_to(spread[0:8, s : s + 1], (8, lz))
+        mix[s] = jnp.broadcast_to(spread[8:16, s : s + 1], (8, lz))
+    end(fh_in.at[0 : n - 1], ph1_r)
+    shrink, widen = 1.0 / stretch(gz), stretch(gz)
+    state = jnp.zeros((8, lz), F32)
+    for s in range(n):
         fin[s] = state
-        return gains(s)[0] * state + fh_in[s]
-
-    end(fh_in.at[0 : n - 1], cst_r)
-    end(fh_in.at[0 : n - 1], ph1_r)
-    lax.fori_loop(0, n, ascend, jnp.zeros((8, lz), F32))
-
-    def descend(k, state):
-        s = n - 1 - k
+        state = gain[s] * state + fh_in[s].astype(F32) * shrink
+    state = jnp.zeros((8, lz), F32)
+    for s in reversed(range(n)):
         entering = fin[s]
-        carry_out[s] = jnp.where(rows8 < CASES, entering, state)
-        gain, mix = gains(s)
-        return gain * state + fh_in[s] + mix * pltpu.roll(entering, CASES, 0)
-
-    lax.fori_loop(0, n, descend, jnp.zeros((8, lz), F32))
+        carry_out[s] = (jnp.where(rows8 < CASES, entering, state) * widen).astype(BF16)
+        state = gain[s] * state + (fh_in[s].astype(F32) * shrink + mix[s] * pltpu.roll(entering, CASES, 0))
     each_far(lambda p: ph2_copy(gz, p).start())
     cx[2 + gz] = carry_out[gz]
     for k in range(others):
@@ -366,6 +366,8 @@
 
     end(fh_in.at[0 : n - 1], ph2_r)
     blocks_copy().start()
+    for p in range(n):
+        cf[2 + p] = cx[2 + p].astype(F32) * inv[p]
     half_y = lax.rem(lane, ly)
     slot = half_y // 4
     for side in range(2):
@@ -373,7 +375,7 @@
         for half in range(2):
             packed = jnp.zeros((8, lz), F32)
             for q in range(n // 2):
-                moved = pltpu.roll(cx[2 + half * (n // 2) + q], (4 * q - y0) % lz, 1)
+                moved = pltpu.roll(cf[2 + half * (n // 2) + q], (4 * q - y0) % lz, 1)
                 packed = jnp.where(slot == q, moved, packed)
             st_out[side, half] = packed
 
@@ -388,16 +390,17 @@
     end(ct_in.at[0 : n - 1], ct_r)
     comp_out[...] = lax.fori_loop(0, n, add_ct, jnp.zeros((1, lz), F32)) * (1.0 / cells)
 
-    for sem in (cst_s, ph1_s, ph2_s):
+    for sem in (ph1_s, ph2_s):
         end(fh_in.at[0 : n - 1], sem)
-    end(ct_in.at[0 : n - 1], ct_s)
+    for sem in (cst_s, ct_s):
+        end(ct_in.at[0 : n - 1], sem)
     for k in range(others):
         cs_copy(k).wait_send()
 
     def along_y(k, _):
         for b in range(4):
             i = k * 4 + b
-            state = cx[2 + i]
+            state = cf[2 + i]
             acc = TAPS[RADIUS] * state
             for t in range(1, RADIUS + 1):
                 down_y = jnp.where(half_y >= t, pltpu.roll(state, t, 1), 0.0)
@@ -411,7 +414,7 @@
     blocks_copy().wait_send()
     blocks_arrive().wait_recv()
     for i in (0, 1, n + 2, n + 3):
-        state = cx[i]
+        state = cx[i].astype(F32) * inv[(i - 2) % n]
         acc = TAPS[RADIUS] * state
         for t in range(1, RADIUS + 1):
             down_y = jnp.where(half_y >= t, pltpu.roll(state, t, 1), 0.0)
@@ -469,40 +472,35 @@
         return 0
 
     lax.fori_loop(0, n // 4, along_x, 0)
-
-
-def last(fm, scale, fc, vmap, comp_in, out_hbm, comp_out, out, sem):
-    lx, ly, lz = fm.shape
     rows_per = lz // ly
-    n = fc.shape[0]
-    step = 4
-    for c in range(CASES):
-        comp_out[c] = jnp.sum(comp_in[0:1, c : c + 1])
-
-    def out_copy(k):
-        rows = pl.ds(k * step * rows_per, step * rows_per)
-        return pltpu.make_async_copy(out.at[rows], out_hbm.at[rows], sem.at[k])
 
     def finish(t, _):
-        for b in range(BATCH * step):
-            p = t * BATCH * step + b
+        for b in range(BATCH):
+            p = t * BATCH + b
             state = fc[p]
             hi = state.astype(BF16).astype(F32)
             stack = jnp.concatenate([hi, state - hi, hi, jnp.zeros((8, lz), F32)], axis=0)
             add = dot(jnp.transpose(stack).astype(BF16), vmap[...], 1, 0).reshape(rows_per, ly, lz)
             at = pl.ds(p * rows_per, rows_per)
-            out[at] = (fm[at] + add) * scale[at]
-        for b in range(BATCH):
-            out_copy(t * BATCH + b).start()
+            fm[at] = (fm[at] + add) * scale[at]
         return 0
 
-    lax.fori_loop(0, n // (BATCH * step), finish, 0)
-
-    def drain_out(k, _):
+    lax.fori_loop(0, n // BATCH, finish, 0)
+
+
+def last(full, comp_in, out_hbm, comp_out, sem):
+    step = full.shape[0] // PIECES
+
+    def out_copy(k):
+        rows = pl.ds(k * step, step)
+        return pltpu.make_async_copy(full.at[rows], out_hbm.at[rows], sem.at[k])
+
+    for k in range(PIECES):
+        out_copy(k).start()
+    for c in range(CASES):
+        comp_out[c] = jnp.sum(comp_in[0:1, c : c + 1])
+    for k in range(PIECES):
         out_copy(k).wait()
-        return 0
-
-    lax.fori_loop(0, n // step, drain_out, 0)
 
 
 def local_step(sizes, density, design_mask, energy, decay, case_index, case_weight):
@@ -515,33 +513,39 @@
     smem = pl.BlockSpec(memory_space=pltpu.SMEM)
     vmem = pl.BlockSpec(memory_space=pltpu.VMEM)
     state = pltpu.VMEM((n, 8, lz), F32)
-    fm, scale, fc, vmap, comp = pl.pallas_call(
+    sent = pltpu.VMEM((n, 8, lz), BF16)
+    full, comp = pl.pallas_call(
         functools.partial(kernel, sizes),
         out_shape=(
             jax.ShapeDtypeStruct((lx, ly, lz), F32),
-            jax.ShapeDtypeStruct((lx, ly, lz), F32),
-            jax.ShapeDtypeStruct((n, 8, lz), F32),
-            jax.ShapeDtypeStruct((32, lz), BF16),
             jax.ShapeDtypeStruct((1, lz), F32),
         ),
         in_specs=[anywhere, anywhere, anywhere, vmem, smem, smem],
-        out_specs=(vmem,) * 5,
+        out_specs=(vmem,) * 2,
         scratch_shapes=[
             pltpu.VMEM((lx, ly, lz), F32),
             pltpu.VMEM((lx, ly, lz), jnp.int32),
             pltpu.VMEM((CASES, lx, ly, lz), BF16),
-            pltpu.VMEM((groups, per, 2 * CASES * lz), BF16),
+            pltpu.VMEM((CASES, lz, lz), F32),
+            pltpu.VMEM((groups, 2 * CASES, per, lz), BF16),
             pltpu.VMEM((2 * CASES * lz, 2 * lz), BF16),
             pltpu.VMEM((32, 2 * CASES * lz), BF16),
             pltpu.VMEM((lx + 2 * RADIUS, ly + 2 * YO, lz), F32),
             pltpu.VMEM((XG, ly + 2 * YO, lz), F32),
-            pltpu.VMEM((8, lz), F32),
+            pltpu.VMEM((lx, ly, lz), F32),
+            state,
+            pltpu.VMEM((32, lz), BF16),
+            state,
+            pltpu.VMEM((n + 4, 8, lz), F32),
+            pltpu.VMEM((1, lz), F32),
+            pltpu.VMEM((n, 1, lz), F32),
             state,
             state,
+            sent,
+            sent,
             state,
-            state,
-            state,
-            pltpu.VMEM((n + 4, 8, lz), F32),
+            sent,
+            pltpu.VMEM((n + 4, 8, lz), BF16),
             pltpu.VMEM((n + 4, 8, lz), F32),
             pltpu.VMEM((n + 4, 8, lz), F32),
             pltpu.VMEM((1, lz), F32),
@@ -592,12 +596,12 @@
             jax.ShapeDtypeStruct((lx, ly, lz), F32),
             jax.ShapeDtypeStruct((CASES,), F32),
         ),
-        in_specs=[vmem] * 5,
+        in_specs=[vmem] * 2,
         out_specs=(anywhere, smem),
-        scratch_shapes=[pltpu.VMEM((lx, ly, lz), F32), dma((n // 4,))],
+        scratch_shapes=[dma((PIECES,))],
         compiler_params=pltpu.CompilerParams(vmem_limit_bytes=20 * 1024 * 1024),
         name="result",
-    )(fm, scale, fc, vmap, comp)
+    )(full, comp)
 
 
 def solution(mesh):

time: 36.7 us -> 33.2 us (0.905)
  Pallas kernels: 35.9 us -> 32.5 us
    pallas_call x1, Pallas kernels: 33.3 us -> 30.6 us  [local_step(): pl.pallas_call(functools.partial(kernel, sizes), out_shape=(jax.ShapeDtyp...]
    pallas_call x1, Pallas kernels: 2.67 us -> 1.89 us  [local_step(): pl.pallas_call(last, out_shape=(jax.ShapeDtypeStruct((lx, ly, lz), F32),...]
where the time goes in v2:
time: 33.2 us; the launch traced here: 33.1 us
  Pallas kernels  32.5 us (98%)
  between operations  0.64 us (2%)
    pallas_call x1, Pallas kernels, local_step(): pl.pallas_call(functools.partial(kernel, sizes), out_shape=(jax.ShapeDtyp...  30.6 us
    pallas_call x1, Pallas kernels, local_step(): pl.pallas_call(last, out_shape=(jax.ShapeDtypeStruct((lx, ly, lz), F32),...  1.89 us

profile of v2, /device:TPU:1, one launch (start us, length us, event | category | flops | bytes accessed | tf_op | source)
XLA Modules:
  0.0 33.1 jit_solution(6154929534903231905)
XLA Ops:
  0.6 30.6 %states.1 = (f32[64,64,128]{2,1,0:T(8,128)S(1)}, f32[1,128]{1,0:T(1,128)S(1)}) custom-call(f32[64,64,128]{2,1,0:T(8,128)} %dens_hbm.1, s32[64,64,128]{2,1,0:T(8,128)} %mask_hbm.1, bf16[4,64,64,128]{3,2,1,0:T(8,128)(2,1)} %en_hbm.1, f32[4,128]{1,0:T(4,128)} %decay_ref.1, s32[4]{0:T(128)} %index_ref.1, f32[16]{0:T(128)} %weight_ref.1), custom_call_target="tpu_custom_call" | custom-call | tf_op jit(solution)/shard_map/states/pallas_call | solution.py:517
  31.2 1.9 %result.1 = (f32[64,64,128]{2,1,0:T(8,128)}, f32[4]{0:T(128)}) custom-call(f32[64,64,128]{2,1,0:T(8,128)S(1)} %get-tuple-element.4.full, f32[1,128]{1,0:T(1,128)S(1)} %get-tuple-element.5.comp_in), custom_call_target="tpu_custom_call" | custom-call | tf_op jit(solution)/shard_map/result/pallas_call | solution.py:593

commit v3 on v2

--- a/solution.py
+++ b/solution.py
@@ -15,7 +15,7 @@
 MESH = pl.DeviceIdType.MESH
 HIGH = lax.Precision.HIGHEST
 XG = 8
-BATCH = 8
+BATCH = 16
 PIECES = 8
 EARLY = 4
 YO = 8
@@ -445,33 +445,22 @@
                     total_y = total_y + jnp.where(lax.rem(lane, 4) == to, TAPS[RADIUS + far] * moved, 0.0)
             st_sum[side, quarter] = total_y
 
-    def add_strips(k, _):
-        for b in range(4):
-            i = k * 4 + b
-            at = i + n // 2 - 2
-            quarter, q = at // (n // 2), lax.rem(at, n // 2)
-            mine_y = slot == q
-            low_y = pltpu.roll(jnp.where(mine_y, st_sum[0, quarter], 0.0), lz - 4 * q, 1)
-            high_y = pltpu.roll(jnp.where(mine_y, st_sum[1, quarter], 0.0), lz + ly - RADIUS - 4 * q, 1)
-            acc = yf[i] + low_y + high_y
-            yf[i] = acc
-            yr[i] = pltpu.roll(acc, ly, 1)
-        return 0
-
-    lax.fori_loop(0, (n + 4) // 4, add_strips, 0)
+    for i in range(n + 4):
+        at = i + n // 2 - 2
+        quarter, q = at // (n // 2), at % (n // 2)
+        mine_y = slot == q
+        low_y = pltpu.roll(jnp.where(mine_y, st_sum[0, quarter], 0.0), (-4 * q) % lz, 1)
+        high_y = pltpu.roll(jnp.where(mine_y, st_sum[1, quarter], 0.0), (ly - RADIUS - 4 * q) % lz, 1)
+        acc = yf[i] + low_y + high_y
+        yf[i] = acc
+        yr[i] = pltpu.roll(acc, ly, 1)
     first_half = lane < ly
-
-    def along_x(k, _):
-        for b in range(4):
-            p = k * 4 + b
-            i = p + 2
-            near = yr[i] + jnp.where(first_half, yr[i - 1], yr[i + 1])
-            far = jnp.where(first_half, yr[i - 2] + yr[i + 1], yr[i - 1] + yr[i + 2])
-            acc = TAPS[RADIUS] * yf[i] + TAPS[RADIUS + 1] * near
-            fc[p] = acc + TAPS[RADIUS + 2] * (yf[i - 1] + yf[i + 1]) + TAPS[RADIUS + 3] * far
-        return 0
-
-    lax.fori_loop(0, n // 4, along_x, 0)
+    for p in range(n):
+        i = p + 2
+        near = yr[i] + jnp.where(first_half, yr[i - 1], yr[i + 1])
+        far = jnp.where(first_half, yr[i - 2] + yr[i + 1], yr[i - 1] + yr[i + 2])
+        acc = TAPS[RADIUS] * yf[i] + TAPS[RADIUS + 1] * near
+        fc[p] = acc + TAPS[RADIUS + 2] * (yf[i - 1] + yf[i + 1]) + TAPS[RADIUS + 3] * far
     rows_per = lz // ly
 
     def finish(t, _):

time: 33.2 us -> 31.6 us (0.952)
  Pallas kernels: 32.5 us -> 30.8 us
    pallas_call x1, Pallas kernels: 30.6 us -> 28.9 us  [local_step(): pl.pallas_call(functools.partial(kernel, sizes), out_shape=(jax.ShapeDtyp...]
where the time goes in v3:
time: 31.6 us; the launch traced here: 31.5 us
  Pallas kernels  30.8 us (97%)
  between operations  0.64 us (2%)
    pallas_call x1, Pallas kernels, local_step(): pl.pallas_call(functools.partial(kernel, sizes), out_shape=(jax.ShapeDtyp...  28.9 us
    pallas_call x1, Pallas kernels, local_step(): pl.pallas_call(last, out_shape=(jax.ShapeDtypeStruct((lx, ly, lz), F32),...  1.89 us

profile of v3, /device:TPU:1, one launch (start us, length us, event | category | flops | bytes accessed | tf_op | source)
XLA Modules:
  0.0 31.5 jit_solution(17944640805855720945)
XLA Ops:
  0.6 28.9 %states.1 = (f32[64,64,128]{2,1,0:T(8,128)S(1)}, f32[1,128]{1,0:T(1,128)S(1)}) custom-call(f32[64,64,128]{2,1,0:T(8,128)} %dens_hbm.1, s32[64,64,128]{2,1,0:T(8,128)} %mask_hbm.1, bf16[4,64,64,128]{3,2,1,0:T(8,128)(2,1)} %en_hbm.1, f32[4,128]{1,0:T(4,128)} %decay_ref.1, s32[4]{0:T(128)} %index_ref.1, f32[16]{0:T(128)} %weight_ref.1), custom_call_target="tpu_custom_call" | custom-call | tf_op jit(solution)/shard_map/states/pallas_call | solution.py:506
  29.6 1.9 %result.1 = (f32[64,64,128]{2,1,0:T(8,128)}, f32[4]{0:T(128)}) custom-call(f32[64,64,128]{2,1,0:T(8,128)S(1)} %get-tuple-element.4.full, f32[1,128]{1,0:T(1,128)S(1)} %get-tuple-element.5.comp_in), custom_call_target="tpu_custom_call" | custom-call | tf_op jit(solution)/shard_map/result/pallas_call | solution.py:582

commit v4 on v3

--- a/solution.py
+++ b/solution.py
@@ -15,7 +15,7 @@
 MESH = pl.DeviceIdType.MESH
 HIGH = lax.Precision.HIGHEST
 XG = 8
-BATCH = 16
+BATCH = 32
 PIECES = 8
 EARLY = 4
 YO = 8

time: 31.6 us -> 31.3 us (level)
  no operation moved by 1% of the time
where the time goes in v4:
time: 31.3 us; the launch traced here: 31.2 us
  Pallas kernels  30.6 us (98%)
  between operations  0.64 us (2%)
    pallas_call x1, Pallas kernels, local_step(): pl.pallas_call(functools.partial(kernel, sizes), out_shape=(jax.ShapeDtyp...  28.7 us
    pallas_call x1, Pallas kernels, local_step(): pl.pallas_call(last, out_shape=(jax.ShapeDtypeStruct((lx, ly, lz), F32),...  1.89 us

profile of v4, /device:TPU:1, one launch (start us, length us, event | category | flops | bytes accessed | tf_op | source)
XLA Modules:
  0.0 31.2 jit_solution(16919910104888607045)
XLA Ops:
  0.6 28.7 %states.1 = (f32[64,64,128]{2,1,0:T(8,128)S(1)}, f32[1,128]{1,0:T(1,128)S(1)}) custom-call(f32[64,64,128]{2,1,0:T(8,128)} %dens_hbm.1, s32[64,64,128]{2,1,0:T(8,128)} %mask_hbm.1, bf16[4,64,64,128]{3,2,1,0:T(8,128)(2,1)} %en_hbm.1, f32[4,128]{1,0:T(4,128)} %decay_ref.1, s32[4]{0:T(128)} %index_ref.1, f32[16]{0:T(128)} %weight_ref.1), custom_call_target="tpu_custom_call" | custom-call | tf_op jit(solution)/shard_map/states/pallas_call | solution.py:506
  29.3 1.9 %result.1 = (f32[64,64,128]{2,1,0:T(8,128)}, f32[4]{0:T(128)}) custom-call(f32[64,64,128]{2,1,0:T(8,128)S(1)} %get-tuple-element.4.full, f32[1,128]{1,0:T(1,128)S(1)} %get-tuple-element.5.comp_in), custom_call_target="tpu_custom_call" | custom-call | tf_op jit(solution)/shard_map/result/pallas_call | solution.py:582
